TPU v7x, 32 devices: a whole 2x2x4 slice. The times are simulated.
32 devices in a mesh: row: 4 (over x, core), col: 8 (over z, y).
Axes of the slice: x: 2, y: 2, z: 4, core: 2. Of those that a mesh axis runs over, the one named last changes fastest.
Arguments:
- rows: bfloat16 [1024, 4096], P(('row', 'col')), may hold values from -6 to 6
- task_ids: int32 [1024], P(('row', 'col')), may hold values from 0 to 8, as said below
- task_embed: bfloat16 [8, 4096], replicated, may hold values from -6 to 6
- norm_gain: float32 [4, 4096], replicated, may hold values from 0.1 to 1.9
- layer_weight: bfloat16 [4, 4096, 4096], P(None, None, 'col'), may hold values from -0.09375 to 0.09375
Outputs:
- packed_out: bfloat16 [1024, 4096], P('row', 'col')
Inputs may be any that keep to these rules, and one draw needn't show every extreme that they name: `task_ids`: 8 marks an empty row, smaller values name a task.
All inputs are finite; a program needn't handle non-finite values.
Results may differ from a plain program's by a relative error of at most 0.008.
Values may be sent and summed in bfloat16 or wider, within the bound.
A program may use at most 128 MiB of HBM per device.

v0:
```python
import jax
import jax.numpy as jnp
from jax import lax
from jax.sharding import PartitionSpec as P

epsilon = 1e-06


def entering(part, axis, combine, identity):
    place = lax.axis_index(axis)
    gathered = lax.all_gather(part, axis)
    state = jnp.zeros_like(part) + jnp.asarray(identity, part.dtype)

    def one(hop, state):
        return combine(state, lax.dynamic_index_in_dim(gathered, hop, 0, False))

    return lax.fori_loop(0, place, one, state)


def add_counts(earlier, later):
    return earlier + later


def activate_rows(hidden, gain):
    total_rows = hidden.shape[0]
    width = hidden.shape[1]
    block_rows = min(512, total_rows)

    def one_block(block):
        values = block.astype(jnp.float32)
        inverse_rms = lax.rsqrt(jnp.mean(values * values, axis=1, keepdims=True) + epsilon)
        return jax.nn.silu(values * inverse_rms * gain[None, :]).astype(jnp.bfloat16)

    blocks = hidden.reshape(total_rows // block_rows, block_rows, width)
    return lax.map(one_block, blocks).reshape(total_rows, width)


def shards(rows, task_ids, task_embed, norm_gain, layer_weight):
    row_count = rows.shape[0]
    width = rows.shape[1]
    task_count = task_embed.shape[0]
    row_devices = lax.axis_size("row")
    col_devices = lax.axis_size("col")
    capacity = row_count // row_devices + task_count
    slots_group = row_count * col_devices
    task_range = jnp.arange(task_count, dtype=jnp.int32)
    member = (task_ids[:, None] == task_range[None, :]).astype(jnp.int32)
    counts = jnp.sum(member, axis=0)
    zero_counts = jnp.zeros_like(counts)
    before_col = entering(counts, "col", add_counts, zero_counts)
    row_total = lax.psum(counts, "col")
    before_row = entering(row_total, "row", add_counts, zero_counts)
    totals = lax.psum(row_total, "row")
    before = before_row + before_col
    task_base = jnp.cumsum(totals) - totals
    positions = jnp.arange(row_count, dtype=jnp.int32)
    earlier_mask = positions[None, :] < positions[:, None]
    same_task = task_ids[:, None] == task_ids[None, :]
    task_rank = jnp.sum((same_task & earlier_mask).astype(jnp.int32), axis=1)
    row_live = task_ids < task_count
    packed_pos = (
        jnp.sum(member * (task_base + before)[None, :], axis=1).astype(jnp.int32) + task_rank
    )
    target_row = packed_pos % row_devices
    slot_index = packed_pos // row_devices
    before_pos = packed_pos[None, :] < packed_pos[:, None]
    same_target = (target_row[:, None] == target_row[None, :]) & row_live[None, :]
    within = jnp.sum((same_target & before_pos).astype(jnp.int32), axis=1)
    send_at = jnp.where(row_live, target_row * capacity + within, -1)
    buffer_range = jnp.arange(row_devices * capacity, dtype=jnp.int32)
    select = buffer_range[:, None] == send_at[None, :]
    send_rows = jnp.dot(
        select.astype(jnp.bfloat16), rows, preferred_element_type=jnp.float32
    ).astype(jnp.bfloat16)
    send_rows = send_rows.reshape(row_devices, capacity, width)
    send_slots = jnp.sum(jnp.where(select, slot_index[None, :] + 1, 0), axis=1) - 1
    send_slots = send_slots.reshape(row_devices, capacity)
    got_rows, got_slots = (
        lax.all_to_all(send_rows, "row", split_axis=0, concat_axis=0, tiled=True),
        lax.all_to_all(send_slots, "row", split_axis=0, concat_axis=0, tiled=True),
    )
    got_rows = got_rows.reshape(row_devices * capacity, width)
    got_slots = got_slots.reshape(row_devices * capacity)
    slot_range = jnp.arange(slots_group, dtype=jnp.int32)
    piece_rows = lax.all_gather(got_rows, "col", axis=0, tiled=True)
    piece_slots = lax.all_gather(got_slots, "col", axis=0, tiled=True)
    safe_slots = jnp.where(piece_slots >= 0, piece_slots, slots_group).astype(jnp.int32)
    placed = (
        jnp.zeros((slots_group, width), jnp.bfloat16).at[safe_slots].set(piece_rows, mode="drop")
    )
    group_index = lax.axis_index("row")
    slot_pos = slot_range * row_devices + group_index
    in_task = (slot_pos[:, None] >= task_base[None, :]) & (
        slot_pos[:, None] < (task_base + totals)[None, :]
    )
    task_term = jnp.dot(
        in_task.astype(jnp.bfloat16), task_embed, preferred_element_type=jnp.float32
    )
    hidden = (placed.astype(jnp.float32) + task_term).astype(jnp.bfloat16)
    part_width = width // col_devices
    column = lax.axis_index("col") * part_width
    layers = layer_weight.shape[0]
    result = hidden
    for layer_index in range(layers):
        active = activate_rows(hidden, norm_gain[layer_index])
        update = jnp.dot(active, layer_weight[layer_index], preferred_element_type=jnp.float32)
        own_cols = lax.dynamic_slice_in_dim(hidden, column, part_width, 1).astype(jnp.float32)
        result = (own_cols + update).astype(jnp.bfloat16)
        if layer_index + 1 < layers:
            hidden = lax.all_gather(result, "col", axis=1, tiled=True)
    return result


def solution(mesh):
    return jax.shard_map(
        shards,
        mesh=mesh,
        in_specs=(P(("row", "col"), None), P(("row", "col")), P(), P(), P(None, None, "col")),
        out_specs=P("row", "col"),
        check_vma=False,
    )
```

profile of v0, /device:TPU:0, one launch (start us, length us, event | category | flops | bytes accessed | tf_op | source)
XLA Modules:
  0.0 303.9 jit_solution(6992512767991493794)
XLA Ops:
  6.5 0.0 copy-start
  6.5 0.0 copy-start.1
  6.5 0.0 all-gather.7.cloned.1.call-start
  6.5 0.8 convert_reduce_fusion.2
  7.4 0.9 convert_reduce_fusion.1
  8.3 0.7 broadcast_compare_fusion
  8.9 1.3 dynamic-slice.5
  10.9 0.2 dynamic-update-slice.1
  11.1 13.1 %all-reduce.3 = (s32[8]{0:T(128)S(1)}, s32[64]{0:T(128)S(1)}) all-reduce(s32[8]{0:T(128)S(1)} %convert_reduce_fusion.2, s32[64]{0:T(128)S(1)} %dynamic-update-slice.1), channel_id=1, replica_groups=mesh['row'=4,'col'=8] {'col'}, use_global_device_ids=true, to_apply=%region_1.2 | all-reduce | flops 72 | bytes 576 | tf_op jit(solution)/shard_map/psum | solution.py:51
  24.2 1.2 dynamic-slice.4
  26.1 0.2 dynamic-update-slice
  26.4 4.9 %all-reduce.4 = (s32[8]{0:T(128)S(1)}, s32[32]{0:T(128)S(1)}) all-reduce(s32[8]{0:T(128)S(1)} %get-tuple-element.117, s32[32]{0:T(128)S(1)} %dynamic-update-slice), channel_id=1, replica_groups=mesh['row'=4,'col'=8] {'row'}, use_global_device_ids=true, to_apply=%region_2.3 | all-reduce | flops 40 | bytes 320 | tf_op jit(solution)/shard_map/psum | solution.py:53
  31.3 0.1 reshape.226
  31.3 0.1 reshape.227
  31.4 0.2 reduce-window.8
  31.6 0.7 select_reduce_fusion.1
  32.4 0.2 convert_reduce_fusion
  32.6 0.7 add_select_fusion
  33.2 0.0 copy-done
  33.2 0.4 convolution_convert_fusion
  33.7 11.9 %all_to_all.11 = bf16[4,16,4096]{2,1,0:T(8,128)(2,1)} all-to-all(bf16[4,16,4096]{2,1,0:T(8,128)(2,1)S(1)} %bitcast.53), channel_id=1, replica_groups=mesh['row'=4,'col'=8] {'row'}, dimensions={0} | all-to-all | bytes 1048576 | tf_op jit(solution)/shard_map/all_to_all | solution.py:79
  45.6 0.0 all-gather.7.cloned.1.call-update
  45.6 0.1 select_reduce_fusion
  45.7 0.7 sub.18
  46.3 3.2 %all-to-all-start = ((s32[4,1,16]{2,1,0:T(1,128)}), s32[4,1,16]{2,1,0:T(1,128)S(1)}, u32[]{:S(2)}, u32[]{:S(2)}) async-start(s32[4,1,16]{2,1,0:T(1,128)} %bitcast.6), calls=%async_computation | async-start | bytes 4096 | tf_op jit(solution)/shard_map/all_to_all | solution.py:80
  49.6 0.0 all-gather.9.cloned.1.call-start
  50.3 1.1 fusion.112
  51.3 1.9 all-to-all-done
  53.2 0.5 broadcast.253
  53.8 0.7 reduce.3
  54.4 0.1 reshape.235
  54.5 0.2 dynamic-update-slice.2
  54.7 9.3 %all-reduce.2 = s32[512]{0:T(512)S(1)} all-reduce(s32[512]{0:T(512)S(1)} %dynamic-update-slice.2), channel_id=1, replica_groups=mesh['row'=4,'col'=8] {'col'}, use_global_device_ids=true, to_apply=%add.2 | all-reduce | flops 512 | bytes 4096
  64.0 52.0 %all-gather.7.cloned.1.call-done = bf16[512,4096]{1,0:T(8,128)(2,1)} async-done(((bf16[64,4096]{1,0:T(8,128)(2,1)}), bf16[512,4096]{1,0:T(8,128)(2,1)}) %all-gather.7.cloned.1.call-update) | async-done | bytes 4194320 | tf_op jit(solution)/shard_map/all_gather | solution.py:85
  116.0 8.2 %scatter_custom_fusion = bf16[256,4096]{1,0:T(8,128)(2,1)S(1)} fusion(s32[512]{0:T(512)S(1)} %compare_select_fusion, bf16[512,4096]{1,0:T(8,128)(2,1)} %all-gather.7.cloned.1.call-done, bf16[]{:T(256)} %constant.131.clone.1), kind=kCustom, calls=%fused_computation.74 | custom fusion | bytes 2097664 | tf_op jit(solution)/shard_map/scatter | solution.py:89
  124.3 0.0 copy-done.1
  124.3 1.0 fusion.1
  125.3 4.4 %fusion.92 = bf16[256,512]{1,0:T(8,128)(2,1)} fusion(bf16[4,4096,512]{2,1,0:T(8,128)(2,1)} %param.13, bf16[256,4096]{1,0:T(8,128)(2,1)S(1)} %get-tuple-element.130, f32[4096]{0:T(1024)S(1)} %bitcast.57, f32[256]{0:T(256)S(1)} %add_rsqrt_fusion.3, s32[]{:T(128)S(6)} %select_n.59), kind=kOutput, calls=%fused_computation.73 | convolution fusion | flops 1082523648 | bytes 6833156 | tf_op jit(solution)/shard_map/dot_general | solution.py:106
  129.7 0.0 all-gather.9.cloned.1.call-update
  129.7 0.2 all-gather.11.cloned.1.call-start
  129.9 48.8 %all-gather.9.cloned.1.call-done = bf16[256,4096]{1,0:T(8,128)(2,1)} async-done(((bf16[256,512]{1,0:T(8,128)(2,1)}), bf16[256,4096]{1,0:T(8,128)(2,1)}) %all-gather.9.cloned.1.call-update) | async-done | bytes 2097168 | tf_op jit(solution)/shard_map/all_gather | solution.py:110
  178.7 2.1 fusion.9
  180.8 5.0 %fusion.87 = bf16[256,512]{1,0:T(8,128)(2,1)} fusion(bf16[4,4096,512]{2,1,0:T(8,128)(2,1)} %param.13, bf16[256,4096]{1,0:T(8,128)(2,1)} %all-gather.9.cloned.1.call-done, f32[4096]{0:T(1024)S(1)} %bitcast.56, f32[256]{0:T(256)S(1)} %add_rsqrt_fusion.2, s32[]{:T(128)S(6)} %select_n.59), kind=kOutput, calls=%fused_computation.72 | convolution fusion | flops 1082523648 | bytes 6833156 | tf_op jit(solution)/shard_map/dot_general | solution.py:106
  185.8 0.0 all-gather.11.cloned.1.call-update
  185.8 0.0 all-gather.13.cloned.1.call-start
  185.8 48.6 %all-gather.11.cloned.1.call-done = bf16[256,4096]{1,0:T(8,128)(2,1)} async-done(((bf16[256,512]{1,0:T(8,128)(2,1)}), bf16[256,4096]{1,0:T(8,128)(2,1)}) %all-gather.11.cloned.1.call-update) | async-done | bytes 2097168 | tf_op jit(solution)/shard_map/all_gather | solution.py:110
  234.5 2.1 fusion.17
  236.6 5.0 %fusion.82 = bf16[256,512]{1,0:T(8,128)(2,1)} fusion(bf16[4,4096,512]{2,1,0:T(8,128)(2,1)} %param.13, bf16[256,4096]{1,0:T(8,128)(2,1)} %all-gather.11.cloned.1.call-done, f32[4096]{0:T(1024)S(1)} %bitcast.55, f32[256]{0:T(256)S(1)} %add_rsqrt_fusion.1, s32[]{:T(128)S(6)} %select_n.59), kind=kOutput, calls=%fused_computation.71 | convolution fusion | flops 1082523648 | bytes 6833156 | tf_op jit(solution)/shard_map/dot_general | solution.py:106
  241.5 0.0 all-gather.13.cloned.1.call-update
  241.6 48.8 %all-gather.13.cloned.1.call-done = bf16[256,4096]{1,0:T(8,128)(2,1)} async-done(((bf16[256,512]{1,0:T(8,128)(2,1)}), bf16[256,4096]{1,0:T(8,128)(2,1)}) %all-gather.13.cloned.1.call-update) | async-done | bytes 2097168 | tf_op jit(solution)/shard_map/all_gather | solution.py:110
  290.3 2.1 fusion.25
  292.4 5.0 %fusion.77 = bf16[256,512]{1,0:T(8,128)(2,1)} fusion(bf16[4,4096,512]{2,1,0:T(8,128)(2,1)} %param.13, bf16[256,4096]{1,0:T(8,128)(2,1)} %all-gather.13.cloned.1.call-done, f32[4096]{0:T(1024)S(1)} %bitcast.54, f32[256]{0:T(256)S(1)} %add_rsqrt_fusion, s32[]{:T(128)S(6)} %select_n.59), kind=kOutput, calls=%fused_computation.70 | convolution fusion | flops 1082523648 | bytes 6833156 | tf_op jit(solution)/shard_map/dot_general | solution.py:106
  (16 shorter events, 0.1 us)
Async XLA Ops:
  6.5 26.7 %copy-start = (bf16[32,4096]{1,0:T(8,128)(2,1)S(1)}, bf16[32,4096]{1,0:T(8,128)(2,1)}, u32[]{:S(2)}) copy-start(bf16[32,4096]{1,0:T(8,128)(2,1)} %param.9) | copy-start | bytes 786436
  6.5 117.7 %copy-start.1 = (bf16[8,4096]{1,0:T(8,128)(2,1)S(1)}, bf16[8,4096]{1,0:T(8,128)(2,1)}, u32[]{:S(2)}) copy-start(bf16[8,4096]{1,0:T(8,128)(2,1)} %param.11) | copy-start | bytes 196612
  6.5 109.5 %all-gather.7.cloned.1.call-start = ((), (), s32[]{:S(2)}) async-start(), calls=%async_computation.2 | async-start | bytes 4718592 | tf_op jit(solution)/shard_map/all_gather | solution.py:85
  46.3 6.9 %all-to-all-start = ((s32[4,1,16]{2,1,0:T(1,128)}), s32[4,1,16]{2,1,0:T(1,128)S(1)}, u32[]{:S(2)}, u32[]{:S(2)}) async-start(s32[4,1,16]{2,1,0:T(1,128)} %bitcast.6), calls=%async_computation | async-start | bytes 4096 | tf_op jit(solution)/shard_map/all_to_all | solution.py:80
  49.6 129.1 %all-gather.9.cloned.1.call-start = ((), (), s32[]{:S(2)}) async-start(), calls=%async_computation.3 | async-start | bytes 2359296 | tf_op jit(solution)/shard_map/all_gather | solution.py:110
  129.7 104.8 %all-gather.11.cloned.1.call-start = ((), (), s32[]{:S(2)}) async-start(), calls=%async_computation.4 | async-start | bytes 2359296 | tf_op jit(solution)/shard_map/all_gather | solution.py:110
  185.8 104.5 %all-gather.13.cloned.1.call-start = ((), (), s32[]{:S(2)}) async-start(), calls=%async_computation.5 | async-start | bytes 2359296 | tf_op jit(solution)/shard_map/all_gather | solution.py:110
Sparse Core Ops, SparseCore 0:
  45.7 70.2 all-gather.6
  129.8 48.8 all-gather.8
  185.9 48.5 all-gather.10
  241.7 48.5 all-gather.12
where the time goes:
time: 304 us
  waiting for transfers between devices  200 us (66%)
  blocking collectives  39.2 us (13%)
  matrix products  20.7 us (7%)
  between operations  15.1 us (5%)
  local copies, waits for them, and re-layouts  13.9 us (5%)
  other arithmetic  11.3 us (4%)
  starting transfers between devices  3.53 us (1%)
    all_gather x3, waiting for transfers between devices, shards(): hidden = lax.all_gather(result, 'col', axis=1, tiled=True)  146 us
    all_gather x1, waiting for transfers between devices, shards(): piece_rows = lax.all_gather(got_rows, 'col', axis=0, tiled=True)  52 us
    dot_general x4, matrix products, shards(): jnp.dot(active, layer_weight[layer_index], preferred_element_type=jnp.flo...  19.3 us
    psum x1, blocking collectives, shards(): row_total = lax.psum(counts, 'col')  13.1 us
    all_to_all x1, blocking collectives, shards(): lax.all_to_all(send_rows, 'row', split_axis=0, concat_axis=0, tiled=True)  11.9 us
    unnamed x1, blocking collectives  9.34 us
    scatter x1, local copies, waits for them, and re-layouts, shards(): jnp.zeros((slots_group, width), jnp.bfloat16).at[safe_slots]  8.22 us
    reduce_sum x3, other arithmetic, one_block(): jnp.mean(values * values, axis=1, keepdims=True) + epsilon  6.25 us
  transfers between devices with their start and end apart: 5, of which 5 were waited for; matrix products, arithmetic and copies ran while one was open for 1% of the time, Pallas kernels for 0%

commit v1 on v0

v1 whole, which is shorter than its diff:
```python
import functools

import jax
import jax.numpy as jnp
from jax import lax
from jax.experimental import pallas as pl
from jax.experimental.pallas import tpu as pltpu
from jax.sharding import PartitionSpec as P

epsilon = 1e-06
MESH = pl.DeviceIdType.MESH
INNER = 2
CHUNKS = 4
LEAD = 1
F32 = jnp.float32
BF16 = jnp.bfloat16


def kernel(
    sizes,
    rows_ref,
    ids_ref,
    embed_ref,
    gain_ref,
    weight_ref,
    out_ref,
    weight,
    hidden,
    active,
    pieces,
    outgo,
    income,
    id_row,
    id_sum,
    id_col,
    sem_weight,
    sem_local,
    send_piece,
    recv_piece,
    send_idrow,
    recv_idrow,
    send_idcol,
    recv_idcol,
    send_row,
    recv_row,
    send_own,
    send_relay,
    recv_hidden,
):
    n_row, n_col, layers, chunks, tasks, cap = sizes
    n_outer = n_col // INNER
    rows_dev = rows_ref.shape[0]
    width = rows_ref.shape[1]
    part = width // n_col
    slots = rows_dev * n_col
    m = slots // chunks
    steps = layers * chunks
    me_r = lax.axis_index("row")
    me_c = lax.axis_index("col")
    outer = me_c // INNER
    inner = me_c % INNER
    partner = outer * INNER + (INNER - 1 - inner)

    def col_peer(j):
        return (me_c + j) % n_col

    def row_peer(j):
        return (me_r + j) % n_row

    def outer_peer(j):
        return ((outer + j) % n_outer) * INNER + inner

    def remote(src, dst, send, recv, r, c):
        return pltpu.make_async_remote_copy(
            src_ref=src, dst_ref=dst, send_sem=send, recv_sem=recv, device_id=(r, c), device_id_type=MESH
        )

    def weight_copy(l):
        return pltpu.make_async_copy(weight_ref.at[l], weight.at[l], sem_weight.at[l])

    barrier = pltpu.get_barrier_semaphore()
    for j in range(1, n_row):
        pl.semaphore_signal(barrier, inc=1, device_id=(row_peer(j), me_c), device_id_type=MESH)
    for j in range(1, n_col):
        pl.semaphore_signal(barrier, inc=1, device_id=(me_r, col_peer(j)), device_id_type=MESH)
    pl.semaphore_wait(barrier, n_row + n_col - 2)

    def id_row_copy(j):
        return remote(ids_ref, id_row.at[me_r], send_idrow.at[j], recv_idrow.at[me_r], row_peer(j), me_c)

    def id_row_from(j):
        return remote(ids_ref, id_row.at[row_peer(j)], send_idrow.at[j], recv_idrow.at[row_peer(j)], row_peer(j), me_c)

    def columns(c):
        return pl.ds(pl.multiple_of(c * part, part), part)

    def piece_copy(j):
        return remote(
            rows_ref.at[:, columns(col_peer(j))], pieces.at[me_c], send_piece.at[j], recv_piece.at[me_c], me_r, col_peer(j)
        )

    def piece_from(j):
        return remote(
            rows_ref.at[:, columns(col_peer(j))], pieces.at[col_peer(j)], send_piece.at[j], recv_piece.at[col_peer(j)],
            me_r, col_peer(j),
        )

    for j in range(1, n_row):
        id_row_copy(j).start()
    for j in range(1, n_col):
        piece_copy(j).start()
    for l in range(layers):
        weight_copy(l).start()
    pieces[me_c] = rows_ref[:, columns(me_c)]

    ids_here = ids_ref[...]
    for j in range(1, n_row):
        id_row_from(j).wait_recv()
        ids_here = ids_here + id_row[row_peer(j)]
    id_sum[...] = ids_here

    def id_col_copy(j):
        return remote(id_sum, id_col.at[me_c], send_idcol.at[j], recv_idcol.at[me_c], me_r, col_peer(j))

    def id_col_from(j):
        return remote(id_sum, id_col.at[col_peer(j)], send_idcol.at[j], recv_idcol.at[col_peer(j)], me_r, col_peer(j))

    for j in range(1, n_col):
        id_col_copy(j).start()
    low = lax.broadcasted_iota(jnp.int32, (slots, slots), 0)
    high = lax.broadcasted_iota(jnp.int32, (slots, slots), 1)
    earlier = jnp.where(low < high, 1.0, 0.0).astype(BF16)
    ids = ids_here
    for j in range(1, n_col):
        id_col_from(j).wait_recv()
        ids = ids + id_col[col_peer(j)]

    lead_dim = ids.shape[0]
    sub = lax.broadcasted_iota(jnp.int32, (lead_dim, slots), 0)
    sub_col = lax.broadcasted_iota(jnp.int32, (lead_dim, 1), 0)
    ids = jnp.where(sub < n_row, ids, tasks)
    live = ids < tasks
    member = [jnp.where(ids == t, 1.0, 0.0) for t in range(tasks)]
    ranks = jnp.dot(jnp.concatenate(member, 0).astype(BF16), earlier, preferred_element_type=F32)
    base = jnp.zeros((1, 1), F32)
    bases, ends = [], []
    position = jnp.zeros((lead_dim, slots), F32)
    for t in range(tasks):
        count = jnp.sum(member[t], axis=1, keepdims=True)
        bases.append(base)
        offset = jnp.zeros((lead_dim, 1), F32) + base
        for r in range(n_row):
            here = count[r : r + 1, :]
            offset = offset + jnp.where(sub_col > r, here, 0.0)
            base = base + here
        ends.append(base)
        rank = ranks[t * lead_dim : (t + 1) * lead_dim, :]
        position = position + member[t] * (offset + rank)
    slot = jnp.floor((position + 0.5) * (1.0 / n_row))
    target = jnp.where(live, position - slot * n_row, -1.0)
    aimed = [jnp.where(target == float(r), 1.0, 0.0) for r in range(n_row)]
    places = jnp.dot(jnp.concatenate(aimed, 0).astype(BF16), earlier, preferred_element_type=F32)
    place = jnp.zeros((lead_dim, slots), F32)
    for r in range(n_row):
        place = place + aimed[r] * places[r * lead_dim : (r + 1) * lead_dim, :]
    slot = slot.astype(jnp.int32)
    target = target.astype(jnp.int32)
    place = place.astype(jnp.int32)

    def of_me(values):
        picked = values[0:1, :]
        for r in range(1, n_row):
            picked = jnp.where(me_r == r, values[r : r + 1, :], picked)
        return picked

    cap_range = lax.broadcasted_iota(jnp.int32, (cap, slots), 0)

    def select(target_row, place_row, r):
        return jnp.where((cap_range == place_row) & (target_row == r), 1.0, 0.0).astype(BF16)

    my_target, my_place = of_me(target), of_me(place)
    picks = [select(my_target, my_place, row_peer(j)) for j in range(n_row)]
    slot_range = lax.broadcasted_iota(jnp.int32, (slots, slots), 0)

    for j in range(1, n_col):
        piece_from(j).wait_recv()
    group = pieces[...].reshape(slots, part)

    def row_copy(j):
        return remote(outgo.at[j], income.at[me_r], send_row.at[j], recv_row.at[me_r], row_peer(j), me_c)

    def row_from(j):
        return remote(outgo.at[j], income.at[row_peer(j)], send_row.at[j], recv_row.at[row_peer(j)], row_peer(j), me_c)

    for j in range(1, n_row):
        outgo[j] = jnp.dot(picks[j], group, preferred_element_type=F32).astype(BF16)
        row_copy(j).start()
    income[me_r] = jnp.dot(picks[0], group, preferred_element_type=F32).astype(BF16)

    puts = []
    for r in range(n_row):
        target_row = target[r : r + 1, :]
        here = jnp.where((slot_range == slot[r : r + 1, :]) & (target_row == me_r), 1.0, 0.0).astype(BF16)
        pick = select(target_row, place[r : r + 1, :], me_r)
        puts.append(
            lax.dot_general(here, pick, (((1,), (1,)), ((), ())), preferred_element_type=F32).astype(BF16)
        )
    slot_pos = (lax.broadcasted_iota(jnp.int32, (slots, 1), 0) * n_row + me_r).astype(F32)
    own_embed = embed_ref[:, columns(me_c)].astype(F32)
    start = jnp.zeros((slots, part), F32)
    for t in range(tasks):
        inside = jnp.where((slot_pos >= bases[t]) & (slot_pos < ends[t]), 1.0, 0.0)
        start = start + inside * own_embed[t : t + 1, :]
    for j in range(1, n_row):
        row_from(j).wait_recv()
    placed = jnp.zeros((slots, part), F32)
    for r in range(n_row):
        placed = placed + jnp.dot(puts[r], income[r], preferred_element_type=F32)
    start = (placed + start).astype(BF16)

    def own_copy(s, peer):
        mine = hidden.at[s, me_c]
        return remote(mine, mine, send_own.at[s % chunks, peer], recv_hidden.at[s, me_c], me_r, peer)

    def relay_copy(s, source):
        block = hidden.at[s, source]
        return remote(block, block, send_relay.at[s % chunks, source], recv_hidden.at[s, source], me_r, partner)

    def arrival(s, source):
        block = hidden.at[s, source]
        return remote(block, block, send_relay.at[s % chunks, source], recv_hidden.at[s, source], me_r, partner)

    def send_all(s):
        for j in range(1, n_outer):
            own_copy(s, outer_peer(j)).start()
        own_copy(s, partner).start()

    def drain_own(s):
        for j in range(1, n_outer):
            own_copy(s, outer_peer(j)).wait_send()
        own_copy(s, partner).wait_send()

    def relay_all(s):
        for j in range(1, n_outer):
            source = outer_peer(j)
            arrival(s, source).wait_recv()
            relay_copy(s, source).start()

    def drain_relay(s):
        for j in range(1, n_outer):
            relay_copy(s, outer_peer(j)).wait_send()

    for ch in range(chunks):
        hidden[ch, me_c] = start[ch * m : (ch + 1) * m, :]
        send_all(ch)
    for s in range(LEAD):
        relay_all(s)

    def step(s, carry):
        l = s // chunks
        ch = s % chunks
        ahead = s + LEAD

        @pl.when(ahead < steps)
        def _():
            @pl.when(ahead >= chunks)
            def _():
                drain_relay(ahead - chunks)

            relay_all(ahead)

        @pl.when(ch == 0)
        def _():
            weight_copy(l).wait()

        arrival(s, partner).wait_recv()
        for j in range(1, n_outer):
            source = ((outer + j) % n_outer) * INNER + (INNER - 1 - inner)
            arrival(s, source).wait_recv()

        total = jnp.zeros((m, part), F32)
        for c in range(n_col):
            values = hidden[s, c].astype(F32)
            total = total + values * values
        mean = jnp.sum(total, axis=1, keepdims=True) * (1.0 / width)
        inverse = lax.rsqrt(mean + epsilon)
        for c in range(n_col):
            cols = slice(c * part, (c + 1) * part)
            values = hidden[s, c].astype(F32) * inverse * gain_ref[l, :, cols]
            half = 0.5 * values
            active[:, cols] = (half + half * jnp.tanh(half)).astype(BF16)
        update = jnp.dot(active[...], weight[l], preferred_element_type=F32)
        result = (hidden[s, me_c].astype(F32) + update).astype(BF16)

        drain_own(s)

        @pl.when(l < layers - 1)
        def _():
            hidden[s + chunks, me_c] = result
            send_all(s + chunks)

        @pl.when(l == layers - 1)
        def _():
            out_ref[ch] = result

        return carry

    lax.fori_loop(0, steps, step, 0)

    for ch in range(chunks):
        drain_relay(steps - chunks + ch)
    for j in range(1, n_row):
        id_row_copy(j).wait_send()
        row_copy(j).wait_send()
    for j in range(1, n_col):
        piece_copy(j).wait_send()
        id_col_copy(j).wait_send()


def shards(rows, task_ids, task_embed, norm_gain, layer_weight):
    rows_dev, width = rows.shape
    tasks = task_embed.shape[0]
    layers = layer_weight.shape[0]
    part = layer_weight.shape[2]
    n_row = lax.axis_size("row")
    n_col = lax.axis_size("col")
    slots = rows_dev * n_col
    cap = -(-(slots // n_row + tasks) // 16) * 16
    chunks = CHUNKS
    m = slots // chunks
    lead_dim = -(-n_row // 8) * 8
    sub = lax.broadcasted_iota(jnp.int32, (lead_dim, slots), 0)
    lane = lax.broadcasted_iota(jnp.int32, (lead_dim, slots), 1)
    own = (sub == lax.axis_index("row")) & (lane // rows_dev == lax.axis_index("col"))
    ids = jnp.where(own, jnp.tile(task_ids, n_col)[None, :], 0)
    sizes = (n_row, n_col, layers, chunks, tasks, cap)
    dma = pltpu.SemaphoreType.DMA
    vmem = pl.BlockSpec(memory_space=pltpu.VMEM)
    out = pl.pallas_call(
        functools.partial(kernel, sizes),
        out_shape=jax.ShapeDtypeStruct((chunks, m, part), BF16),
        in_specs=[vmem, vmem, vmem, vmem, pl.BlockSpec(memory_space=pl.ANY)],
        out_specs=vmem,
        scratch_shapes=[
            pltpu.VMEM((layers, width, part), BF16),
            pltpu.VMEM((layers * chunks, n_col, m, part), BF16),
            pltpu.VMEM((m, width), BF16),
            pltpu.VMEM((n_col, rows_dev, part), BF16),
            pltpu.VMEM((n_row, cap, part), BF16),
            pltpu.VMEM((n_row, cap, part), BF16),
            pltpu.VMEM((n_row, lead_dim, slots), jnp.int32),
            pltpu.VMEM((lead_dim, slots), jnp.int32),
            pltpu.VMEM((n_col, lead_dim, slots), jnp.int32),
            dma((layers,)),
            dma,
            dma((n_col,)),
            dma((n_col,)),
            dma((n_row,)),
            dma((n_row,)),
            dma((n_col,)),
            dma((n_col,)),
            dma((n_row,)),
            dma((n_row,)),
            dma((chunks, n_col)),
            dma((chunks, n_col)),
            dma((layers * chunks, n_col)),
        ],
        compiler_params=pltpu.CompilerParams(
            collective_id=0, has_side_effects=True, vmem_limit_bytes=60 * 1024 * 1024
        ),
    )(rows, ids, task_embed, norm_gain.reshape(layers, 1, width), layer_weight)
    return out.reshape(slots, part)


def solution(mesh):
    return jax.shard_map(
        shards,
        mesh=mesh,
        in_specs=(P(("row", "col"), None), P(("row", "col")), P(), P(), P(None, None, "col")),
        out_specs=P("row", "col"),
        check_vma=False,
    )
```

time: 304 us -> 130 us (0.43)
  the two profiles are of different devices: /device:TPU:0 before, /device:TPU:24 now
where the time goes in v1:
time: 130 us; the launch traced here: 129 us
  Pallas kernels  125 us (96%)
  local copies, waits for them, and re-layouts  3.92 us (3%)
    pallas_call x1, Pallas kernels, shards(): pl.pallas_call(functools.partial(kernel, sizes), out_shape=jax.ShapeDtype...  125 us

profile of v1, /device:TPU:24, one launch (start us, length us, event | category | flops | bytes accessed | tf_op | source)
XLA Modules:
  0.0 129.4 jit_solution(2879258218956249437)
XLA Ops:
  0.0 0.7 tile.2
  0.7 0.1 broadcast_in_dim.12
  0.8 0.7 fusion.1.ids_ref
  1.4 1.5 %reshape.8.gain_ref = f32[4,1,4096]{2,1,0:T(1,128)} reshape(f32[4,4096]{1,0:T(4,128)} %param.8) | data formatting | bytes 131072 | tf_op jit(solution)/shard_map/reshape | solution.py:371
  2.9 124.8 %shard_map.55 = bf16[4,64,512]{2,1,0:T(8,128)(2,1)} custom-call(bf16[32,4096]{1,0:T(8,128)(2,1)} %rows_ref.1, s32[8,256]{1,0:T(8,128)} %fusion.1.ids_ref, bf16[8,4096]{1,0:T(8,128)(2,1)} %embed_ref.1, f32[4,1,4096]{2,1,0:T(1,128)} %reshape.8.gain_ref, bf16[4,4096,512]{2,1,0:T(8,128)(2,1)} %weight_ref.1), custom_call_target="tpu_custom_call" | custom-call | tf_op jit(solution)/shard_map/pallas_call | solution.py:339
  127.7 1.7 %copy.7 = bf16[256,512]{1,0:T(8,128)(2,1)} copy(bf16[256,512]{1,0:T(8,128)(2,1)} %bitcast.1) | data formatting | bytes 524288
  (3 shorter events, 0.0 us)

commit v2 on v1

--- a/solution.py
+++ b/solution.py
@@ -11,7 +11,8 @@
 MESH = pl.DeviceIdType.MESH
 INNER = 2
 CHUNKS = 4
-LEAD = 1
+LEAD1 = 2
+LEAD2 = 1
 F32 = jnp.float32
 BF16 = jnp.bfloat16
 
@@ -27,14 +28,15 @@
     weight,
     hidden,
     active,
+    gain,
     pieces,
     outgo,
     income,
+    id_own,
     id_row,
     id_sum,
     id_col,
     sem_weight,
-    sem_local,
     send_piece,
     recv_piece,
     send_idrow,
@@ -45,6 +47,7 @@
     recv_row,
     send_own,
     send_relay,
+    send_along,
     recv_hidden,
 ):
     n_row, n_col, layers, chunks, tasks, cap = sizes
@@ -78,6 +81,16 @@
     def weight_copy(l):
         return pltpu.make_async_copy(weight_ref.at[l], weight.at[l], sem_weight.at[l])
 
+    lead_dim = id_own.shape[0]
+    spread = lax.broadcasted_iota(jnp.int32, (rows_dev, slots), 1) - lax.broadcasted_iota(
+        jnp.int32, (rows_dev, slots), 0
+    )
+    spread = jnp.where(spread == me_c * rows_dev, 1.0, 0.0).astype(BF16)
+    own_ids = jnp.broadcast_to(ids_ref[...].astype(F32), (lead_dim, rows_dev)).astype(BF16)
+    own_ids = jnp.dot(own_ids, spread, preferred_element_type=F32).astype(jnp.int32)
+    sub = lax.broadcasted_iota(jnp.int32, (lead_dim, slots), 0)
+    id_own[...] = jnp.where(sub == me_r, own_ids, 0)
+
     barrier = pltpu.get_barrier_semaphore()
     for j in range(1, n_row):
         pl.semaphore_signal(barrier, inc=1, device_id=(row_peer(j), me_c), device_id_type=MESH)
@@ -86,10 +99,10 @@
     pl.semaphore_wait(barrier, n_row + n_col - 2)
 
     def id_row_copy(j):
-        return remote(ids_ref, id_row.at[me_r], send_idrow.at[j], recv_idrow.at[me_r], row_peer(j), me_c)
+        return remote(id_own, id_row.at[me_r], send_idrow.at[j], recv_idrow.at[me_r], row_peer(j), me_c)
 
     def id_row_from(j):
-        return remote(ids_ref, id_row.at[row_peer(j)], send_idrow.at[j], recv_idrow.at[row_peer(j)], row_peer(j), me_c)
+        return remote(id_own, id_row.at[row_peer(j)], send_idrow.at[j], recv_idrow.at[row_peer(j)], row_peer(j), me_c)
 
     def columns(c):
         return pl.ds(pl.multiple_of(c * part, part), part)
@@ -112,8 +125,10 @@
     for l in range(layers):
         weight_copy(l).start()
     pieces[me_c] = rows_ref[:, columns(me_c)]
-
-    ids_here = ids_ref[...]
+    for l in range(layers):
+        gain[l] = gain_ref[l : l + 1, :]
+
+    ids_here = id_own[...]
     for j in range(1, n_row):
         id_row_from(j).wait_recv()
         ids_here = ids_here + id_row[row_peer(j)]
@@ -135,8 +150,6 @@
         id_col_from(j).wait_recv()
         ids = ids + id_col[col_peer(j)]
 
-    lead_dim = ids.shape[0]
-    sub = lax.broadcasted_iota(jnp.int32, (lead_dim, slots), 0)
     sub_col = lax.broadcasted_iota(jnp.int32, (lead_dim, 1), 0)
     ids = jnp.where(sub < n_row, ids, tasks)
     live = ids < tasks
@@ -218,66 +231,118 @@
         placed = placed + jnp.dot(puts[r], income[r], preferred_element_type=F32)
     start = (placed + start).astype(BF16)
 
-    def own_copy(s, peer):
-        mine = hidden.at[s, me_c]
-        return remote(mine, mine, send_own.at[s % chunks, peer], recv_hidden.at[s, me_c], me_r, peer)
-
-    def relay_copy(s, source):
+    half = n_outer // 2
+    side = outer // half
+    is_gate = outer == half - 1 + side
+    far_gate = (half - side) * INNER + inner
+
+    def near(j, i):
+        return (side * half + (outer % half + j) % half) * INNER + i
+
+    def far(k, i):
+        return ((1 - side) * half + k) * INNER + i
+
+    other = INNER - 1 - inner
+
+    def block_copy(s, source, send, peer):
         block = hidden.at[s, source]
-        return remote(block, block, send_relay.at[s % chunks, source], recv_hidden.at[s, source], me_r, partner)
-
-    def arrival(s, source):
-        block = hidden.at[s, source]
-        return remote(block, block, send_relay.at[s % chunks, source], recv_hidden.at[s, source], me_r, partner)
+        return remote(block, block, send, recv_hidden.at[s, source], me_r, peer)
+
+    def await_block(s, source):
+        block_copy(s, source, send_relay.at[0, source], partner).wait_recv()
+
+    def own_copies(s):
+        peers = [near(j, inner) for j in range(1, half)] + [far_gate, partner]
+        return [block_copy(s, me_c, send_own.at[s % chunks, peer], peer) for peer in peers]
 
     def send_all(s):
-        for j in range(1, n_outer):
-            own_copy(s, outer_peer(j)).start()
-        own_copy(s, partner).start()
+        for copy in own_copies(s):
+            copy.start()
 
     def drain_own(s):
-        for j in range(1, n_outer):
-            own_copy(s, outer_peer(j)).wait_send()
-        own_copy(s, partner).wait_send()
-
-    def relay_all(s):
-        for j in range(1, n_outer):
-            source = outer_peer(j)
-            arrival(s, source).wait_recv()
-            relay_copy(s, source).start()
-
-    def drain_relay(s):
-        for j in range(1, n_outer):
-            relay_copy(s, outer_peer(j)).wait_send()
+        for copy in own_copies(s):
+            copy.wait_send()
+
+    def over(s, source):
+        return block_copy(s, source, send_relay.at[s % chunks, source], partner)
+
+    def along(s, source, j):
+        return block_copy(s, source, send_along.at[s % chunks, source // INNER, j], near(j, inner))
+
+    def pass_on(s, go, source, copies):
+        if go:
+            await_block(s, source)
+        for copy in copies:
+            if go:
+                copy.start()
+            else:
+                copy.wait_send()
+
+    def first_relay(s, go):
+        @pl.when(is_gate)
+        def _():
+            for k in range(half):
+                source = far(k, inner)
+                pass_on(s, go, source, [along(s, source, j) for j in range(1, half)] + [over(s, source)])
+
+        @pl.when(s % 2 == 0)
+        def _():
+            for j in range(1, half):
+                pass_on(s, go, near(j, inner), [over(s, near(j, inner))])
+
+        @pl.when(s % 2 == 1)
+        def _():
+            pass_on(s, go, partner, [along(s, partner, j) for j in range(1, half)])
+
+    def second_relay(s, go):
+        @pl.when(jnp.logical_not(is_gate))
+        def _():
+            for k in range(half):
+                pass_on(s, go, far(k, inner), [over(s, far(k, inner))])
+
+    def await_rest(s):
+        @pl.when(s % 2 == 0)
+        def _():
+            await_block(s, partner)
+
+        @pl.when(s % 2 == 1)
+        def _():
+            for j in range(1, half):
+                await_block(s, near(j, inner))
+
+        for j in range(1, half):
+            await_block(s, near(j, other))
+        for k in range(half):
+            await_block(s, far(k, other))
+
+    def relay(s, relay_of):
+        @pl.when(s < steps)
+        def _():
+            @pl.when(s >= chunks)
+            def _():
+                relay_of(s - chunks, False)
+
+            relay_of(s, True)
 
     for ch in range(chunks):
         hidden[ch, me_c] = start[ch * m : (ch + 1) * m, :]
         send_all(ch)
-    for s in range(LEAD):
-        relay_all(s)
+    for s in range(LEAD1):
+        first_relay(jnp.int32(s), True)
+    for s in range(LEAD2):
+        second_relay(jnp.int32(s), True)
 
     def step(s, carry):
         l = s // chunks
         ch = s % chunks
-        ahead = s + LEAD
-
-        @pl.when(ahead < steps)
-        def _():
-            @pl.when(ahead >= chunks)
-            def _():
-                drain_relay(ahead - chunks)
-
-            relay_all(ahead)
+        relay(s + LEAD2, second_relay)
+        relay(s + LEAD1, first_relay)
 
         @pl.when(ch == 0)
         def _():
             weight_copy(l).wait()
 
-        arrival(s, partner).wait_recv()
-        for j in range(1, n_outer):
-            source = ((outer + j) % n_outer) * INNER + (INNER - 1 - inner)
-            arrival(s, source).wait_recv()
-
+        await_rest(s)
         total = jnp.zeros((m, part), F32)
         for c in range(n_col):
             values = hidden[s, c].astype(F32)
@@ -286,7 +351,7 @@
         inverse = lax.rsqrt(mean + epsilon)
         for c in range(n_col):
             cols = slice(c * part, (c + 1) * part)
-            values = hidden[s, c].astype(F32) * inverse * gain_ref[l, :, cols]
+            values = hidden[s, c].astype(F32) * inverse * gain[l, :, cols]
             half = 0.5 * values
             active[:, cols] = (half + half * jnp.tanh(half)).astype(BF16)
         update = jnp.dot(active[...], weight[l], preferred_element_type=F32)
@@ -308,7 +373,8 @@
     lax.fori_loop(0, steps, step, 0)
 
     for ch in range(chunks):
-        drain_relay(steps - chunks + ch)
+        first_relay(jnp.int32(steps - chunks + ch), False)
+        second_relay(jnp.int32(steps - chunks + ch), False)
     for j in range(1, n_row):
         id_row_copy(j).wait_send()
         row_copy(j).wait_send()
@@ -329,10 +395,6 @@
     chunks = CHUNKS
     m = slots // chunks
     lead_dim = -(-n_row // 8) * 8
-    sub = lax.broadcasted_iota(jnp.int32, (lead_dim, slots), 0)
-    lane = lax.broadcasted_iota(jnp.int32, (lead_dim, slots), 1)
-    own = (sub == lax.axis_index("row")) & (lane // rows_dev == lax.axis_index("col"))
-    ids = jnp.where(own, jnp.tile(task_ids, n_col)[None, :], 0)
     sizes = (n_row, n_col, layers, chunks, tasks, cap)
     dma = pltpu.SemaphoreType.DMA
     vmem = pl.BlockSpec(memory_space=pltpu.VMEM)
@@ -345,14 +407,15 @@
             pltpu.VMEM((layers, width, part), BF16),
             pltpu.VMEM((layers * chunks, n_col, m, part), BF16),
             pltpu.VMEM((m, width), BF16),
+            pltpu.VMEM((layers, 1, width), F32),
             pltpu.VMEM((n_col, rows_dev, part), BF16),
             pltpu.VMEM((n_row, cap, part), BF16),
             pltpu.VMEM((n_row, cap, part), BF16),
+            pltpu.VMEM((lead_dim, slots), jnp.int32),
             pltpu.VMEM((n_row, lead_dim, slots), jnp.int32),
             pltpu.VMEM((lead_dim, slots), jnp.int32),
             pltpu.VMEM((n_col, lead_dim, slots), jnp.int32),
             dma((layers,)),
-            dma,
             dma((n_col,)),
             dma((n_col,)),
             dma((n_row,)),
@@ -363,12 +426,13 @@
             dma((n_row,)),
             dma((chunks, n_col)),
             dma((chunks, n_col)),
+            dma((chunks, n_col // INNER, max(1, n_col // INNER // 2))),
             dma((layers * chunks, n_col)),
         ],
         compiler_params=pltpu.CompilerParams(
             collective_id=0, has_side_effects=True, vmem_limit_bytes=60 * 1024 * 1024
         ),
-    )(rows, ids, task_embed, norm_gain.reshape(layers, 1, width), layer_weight)
+    )(rows, task_ids.reshape(1, rows_dev), task_embed, norm_gain, layer_weight)
     return out.reshape(slots, part)
 
 

time: 130 us -> 110 us (0.85)
  the two profiles are of different devices: /device:TPU:24 before, /device:TPU:0 now
where the time goes in v2:
time: 110 us
  Pallas kernels  108 us (98%)
  local copies, waits for them, and re-layouts  1.67 us (2%)
    pallas_call x1, Pallas kernels, shards(): pl.pallas_call(functools.partial(kernel, sizes), out_shape=jax.ShapeDtype...  108 us

profile of v2, /device:TPU:0, one launch (start us, length us, event | category | flops | bytes accessed | tf_op | source)
XLA Modules:
  0.0 109.9 jit_solution(14534651202394009326)
XLA Ops:
  0.0 108.2 %shard_map.55 = bf16[4,64,512]{2,1,0:T(8,128)(2,1)} custom-call(bf16[32,4096]{1,0:T(8,128)(2,1)} %rows_ref.1, s32[1,32]{1,0:T(1,128)} %bitcast.3, bf16[8,4096]{1,0:T(8,128)(2,1)} %embed_ref.1, f32[4,4096]{1,0:T(4,128)} %gain_ref.1, bf16[4,4096,512]{2,1,0:T(8,128)(2,1)} %weight_ref.1), custom_call_target="tpu_custom_call" | custom-call | tf_op jit(solution)/shard_map/pallas_call | solution.py:401
  108.2 1.7 %copy.7 = bf16[256,512]{1,0:T(8,128)(2,1)} copy(bf16[256,512]{1,0:T(8,128)(2,1)} %bitcast.2) | data formatting | bytes 524288

commit v3 on v2

--- a/solution.py
+++ b/solution.py
@@ -226,10 +226,6 @@
         start = start + inside * own_embed[t : t + 1, :]
     for j in range(1, n_row):
         row_from(j).wait_recv()
-    placed = jnp.zeros((slots, part), F32)
-    for r in range(n_row):
-        placed = placed + jnp.dot(puts[r], income[r], preferred_element_type=F32)
-    start = (placed + start).astype(BF16)
 
     half = n_outer // 2
     side = outer // half
@@ -325,7 +321,11 @@
             relay_of(s, True)
 
     for ch in range(chunks):
-        hidden[ch, me_c] = start[ch * m : (ch + 1) * m, :]
+        span = slice(ch * m, (ch + 1) * m)
+        placed = jnp.zeros((m, part), F32)
+        for r in range(n_row):
+            placed = placed + jnp.dot(puts[r][span, :], income[r], preferred_element_type=F32)
+        hidden[ch, me_c] = (placed + start[span, :]).astype(BF16)
         send_all(ch)
     for s in range(LEAD1):
         first_relay(jnp.int32(s), True)

time: 110 us -> 110 us (level)
  no operation moved by 1% of the time
where the time goes in v3:
time: 110 us
  Pallas kernels  108 us (98%)
  local copies, waits for them, and re-layouts  1.67 us (2%)
    pallas_call x1, Pallas kernels, shards(): pl.pallas_call(functools.partial(kernel, sizes), out_shape=jax.ShapeDtype...  108 us

profile of v3, /device:TPU:0, one launch (start us, length us, event | category | flops | bytes accessed | tf_op | source)
XLA Modules:
  0.0 109.7 jit_solution(5842373773715598019)
XLA Ops:
  0.0 108.0 %shard_map.55 = bf16[4,64,512]{2,1,0:T(8,128)(2,1)} custom-call(bf16[32,4096]{1,0:T(8,128)(2,1)} %rows_ref.1, s32[1,32]{1,0:T(1,128)} %bitcast.3, bf16[8,4096]{1,0:T(8,128)(2,1)} %embed_ref.1, f32[4,4096]{1,0:T(4,128)} %gain_ref.1, bf16[4,4096,512]{2,1,0:T(8,128)(2,1)} %weight_ref.1), custom_call_target="tpu_custom_call" | custom-call | tf_op jit(solution)/shard_map/pallas_call | solution.py:401
  108.0 1.7 %copy.7 = bf16[256,512]{1,0:T(8,128)(2,1)} copy(bf16[256,512]{1,0:T(8,128)(2,1)} %bitcast.2) | data formatting | bytes 524288
